TPU v7x, 32 devices: a whole 2x2x4 slice. The times are simulated.
32 devices in a mesh: seq: 2 (over x), row: 4 (over y, core), col: 4 (over z).
Axes of the slice: x: 2, y: 2, z: 4, core: 2. Of those that a mesh axis runs over, the one named last changes fastest.
Arguments:
- activations: bfloat16 [2, 64, 8192], P(None, 'row', 'seq'), may hold values from -6 to 6
- gradients: bfloat16 [2, 64, 8192], P(None, 'col', 'seq'), may hold values from -6 to 6
- basis_in: bfloat16 [8192, 4096], P('seq', 'col'), may hold values from -0.0625 to 0.0625
- basis_out: bfloat16 [8192, 4096], P('seq', 'row'), may hold values from -0.0625 to 0.0625
- lengths: int32 [2], replicated, may hold values from 16 to 64
Outputs:
- corrections: float32 [4096, 4096], P(('row', 'seq'), 'col')
All inputs are finite; a program needn't handle non-finite values.
Results may differ from a plain program's by a relative error of at most 0.0023.
Values may be sent and summed in bfloat16 or wider, within the bound.
No kernel may reach another device: no remote copies, remote signals or barrier semaphores. Data moves between devices by JAX's collectives and lax.ppermute only.
A program may use at most 64 MiB of HBM per device.

v0:
```python
import jax
import jax.numpy as jnp
from jax import lax
from jax.sharding import PartitionSpec as P


def turned_terms(tokens, basis):
    return jnp.einsum("ntf,fk->ntk", tokens, basis, preferred_element_type=jnp.float32)


def local(activations, gradients, basis_in, basis_out, lengths):
    seq_count = lax.axis_size("seq")
    seq_index = lax.axis_index("seq")
    length = lengths[seq_index]
    summed_in = lax.psum_scatter(
        turned_terms(activations, basis_in), "seq", scatter_dimension=0, tiled=True
    )
    turned_in = summed_in[0].astype(jnp.bfloat16)
    summed_out = lax.psum_scatter(
        turned_terms(gradients, basis_out), "seq", scatter_dimension=0, tiled=True
    )
    turned_out = summed_out[0].astype(jnp.bfloat16)
    every_in = lax.all_gather(turned_in, "row", axis=0, tiled=True)
    every_out = lax.all_gather(turned_out, "col", axis=0, tiled=True)
    slot_total = every_in.shape[0]
    slots = jnp.arange(slot_total)
    contract = (((0,), (0,)), ((), ()))
    kept = jnp.where((slots < length)[:, None], every_out, jnp.zeros((), jnp.bfloat16))
    product_tile = lax.dot_general(kept, every_in, contract, preferred_element_type=jnp.float32)
    squared = product_tile * product_tile / (seq_count * slot_total)
    return lax.psum_scatter(squared, "seq", scatter_dimension=0, tiled=True)


def solution(mesh):
    return jax.shard_map(
        local,
        mesh=mesh,
        in_specs=(
            P(None, "row", "seq"),
            P(None, "col", "seq"),
            P("seq", "col"),
            P("seq", "row"),
            P(),
        ),
        out_specs=P(("row", "seq"), "col"),
        check_vma=False,
    )
```

profile of v0, /device:TPU:0, one launch (start us, length us, event | category | flops | bytes accessed | tf_op | source)
XLA Modules:
  0.0 117.2 jit_solution(11242291318039714321)
XLA Ops:
  6.5 0.0 copy-start
  6.5 0.0 copy-start.1
  6.5 0.0 reduce-scatter.6.cloned.1.call-start
  6.5 0.9 copy-done
  7.5 5.6 %fusion = f32[2,16,1024]{2,1,0:T(8,128)} fusion(bf16[2,16,4096]{2,1,0:T(8,128)(2,1)S(1)} %copy-done, bf16[4096,1024]{1,0:T(8,128)(2,1)} %param.7), kind=kOutput, calls=%fused_computation | convolution fusion | flops 268435456 | bytes 8781824 | tf_op jit(solution)/shard_map/ntf,fk->ntk/dot_general | solution.py:8
  13.1 0.0 copy-start.2
  13.1 0.0 reduce-scatter.6.cloned.1.call-update
  13.1 0.0 reduce-scatter.4.cloned.1.call-start
  13.1 0.0 copy-done.1
  13.2 5.6 %fusion.2 = f32[2,16,1024]{2,1,0:T(8,128)} fusion(bf16[2,16,4096]{2,1,0:T(8,128)(2,1)S(1)} %copy-done.1, bf16[4096,1024]{1,0:T(8,128)(2,1)} %param.8), kind=kOutput, calls=%fused_computation.2 | convolution fusion | flops 268435456 | bytes 8781824 | tf_op jit(solution)/shard_map/ntf,fk->ntk/dot_general | solution.py:8
  18.7 0.0 reduce-scatter.4.cloned.1.call-update
  18.8 0.0 reduce-scatter.8.cloned.1.call-start
  18.8 0.0 copy-done.2
  18.8 0.7 dynamic_slice.3
  19.5 0.7 iota_compare_fusion
  20.2 6.1 %reduce-scatter.6.cloned.1.call-done = f32[1,16,1024]{2,1,0:T(8,128)} async-done(((f32[2,16,1024]{2,1,0:T(8,128)}), f32[1,16,1024]{2,1,0:T(8,128)}) %reduce-scatter.6.cloned.1.call-update) | async-done | bytes 65552 | tf_op jit(solution)/shard_map/reduce_scatter | solution.py:15
  26.3 0.8 convert_element_type.14
  27.2 5.4 %all-gather.1 = bf16[1,64,1024]{2,1,0:T(8,128)(2,1)S(1)} all-gather(bf16[1,16,1024]{2,1,0:T(8,128)(2,1)S(1)} %convert_element_type.14), channel_id=3, replica_groups=mesh['seq'=2,'row'=4,'col'=4] {'row'}, dimensions={1}, use_global_device_ids=true | all-gather | bytes 163840 | tf_op jit(solution)/shard_map/all_gather | solution.py:23
  32.6 6.4 %reduce-scatter.4.cloned.1.call-done = f32[1,16,1024]{2,1,0:T(8,128)} async-done(((f32[2,16,1024]{2,1,0:T(8,128)}), f32[1,16,1024]{2,1,0:T(8,128)}) %reduce-scatter.4.cloned.1.call-update) | async-done | bytes 65552 | tf_op jit(solution)/shard_map/reduce_scatter | solution.py:19
  38.9 0.8 convert_element_type.12
  39.8 13.4 %all-gather = bf16[1,64,1024]{2,1,0:T(8,128)(2,1)S(1)} all-gather(bf16[1,16,1024]{2,1,0:T(8,128)(2,1)S(1)} %convert_element_type.12), channel_id=2, replica_groups=mesh['seq'=2,'row'=4,'col'=4] {'col'}, dimensions={1}, use_global_device_ids=true | all-gather | bytes 163840 | tf_op jit(solution)/shard_map/all_gather | solution.py:24
  53.2 2.8 %multiply_multiply_fusion = f32[1024,1024]{1,0:T(8,128)} fusion(bf16[1,64,1024]{2,1,0:T(8,128)(2,1)S(1)} %all-gather.1, bf16[1,64,1024]{2,1,0:T(8,128)(2,1)S(1)} %all-gather, pred[64]{0:T(512)(128)(4,1)S(1)} %iota_compare_fusion), kind=kOutput, calls=%fused_computation.4 | convolution fusion | flops 136380416 | bytes 4456512 | tf_op jit(solution)/shard_map/dot_general | solution.py:29
  56.0 0.0 reduce-scatter.8.cloned.1.call-update
  56.0 54.7 %reduce-scatter.8.cloned.1.call-done = f32[512,1024]{1,0:T(8,128)} async-done(((f32[1024,1024]{1,0:T(8,128)}), f32[512,1024]{1,0:T(8,128)}) %reduce-scatter.8.cloned.1.call-update) | async-done | bytes 2097168 | tf_op jit(solution)/shard_map/reduce_scatter | solution.py:31
Async XLA Ops:
  6.5 1.0 copy-start
  6.5 6.6 %copy-start.1 = (bf16[2,16,4096]{2,1,0:T(8,128)(2,1)S(1)}, bf16[2,16,4096]{2,1,0:T(8,128)(2,1)}, u32[]{:S(2)}) copy-start(bf16[2,16,4096]{2,1,0:T(8,128)(2,1)} %param.6) | copy-start | bytes 786436
  6.5 19.8 %reduce-scatter.6.cloned.1.call-start = ((), (), s32[]{:S(2)}) async-start(), calls=%async_computation.4 | async-start | bytes 196608 | tf_op jit(solution)/shard_map/reduce_scatter | solution.py:15
  13.1 5.7 %copy-start.2 = (s32[2]{0:T(128)S(1)}, s32[2]{0:T(128)}, u32[]{:S(2)}) copy-start(s32[2]{0:T(128)} %param.9) | copy-start | bytes 28
  13.1 25.8 %reduce-scatter.4.cloned.1.call-start = ((), (), s32[]{:S(2)}) async-start(), calls=%async_computation.3 | async-start | bytes 196608 | tf_op jit(solution)/shard_map/reduce_scatter | solution.py:19
  18.8 92.0 %reduce-scatter.8.cloned.1.call-start = ((), (), s32[]{:S(2)}) async-start(), calls=%async_computation.5 | async-start | bytes 6291456 | tf_op jit(solution)/shard_map/reduce_scatter | solution.py:31
Sparse Core Ops, SparseCore 0:
  13.2 13.0 reduce-scatter.5
  28.5 10.3 reduce-scatter.3
  56.1 54.5 reduce-scatter.7
where the time goes:
time: 118 us; the launch traced here: 117 us
  waiting for transfers between devices  67.3 us (57%)
  blocking collectives  18.8 us (16%)
  matrix products  13.9 us (12%)
  between operations  13.1 us (11%)
  other arithmetic  2.38 us (2%)
  local copies, waits for them, and re-layouts  1.62 us (1%)
    reduce_scatter x1, waiting for transfers between devices, local(): return lax.psum_scatter(squared, 'seq', scatter_dimension=0, tiled=True)  54.7 us
    all_gather x1, blocking collectives, local(): every_out = lax.all_gather(turned_out, 'col', axis=0, tiled=True)  13.4 us
    dot_general x2, matrix products, turned_terms(): jnp.einsum('ntf,fk->ntk', tokens, basis, preferred_element_type=jnp.float32)  11.2 us
    reduce_scatter x1, waiting for transfers between devices, local(): lax.psum_scatter(turned_terms(gradients, basis_out), 'seq', scatter_dimen...  6.36 us
    reduce_scatter x1, waiting for transfers between devices, local(): lax.psum_scatter(turned_terms(activations, basis_in), 'seq', scatter_dime...  6.15 us
    all_gather x1, blocking collectives, local(): every_in = lax.all_gather(turned_in, 'row', axis=0, tiled=True)  5.4 us
    dot_general x1, matrix products, local(): lax.dot_general(kept, every_in, contract, preferred_element_type=jnp.floa...  2.75 us
  transfers between devices with their start and end apart: 3, of which 3 were waited for; matrix products, arithmetic and copies ran while one was open for 7% of the time, Pallas kernels for 0%

commit v1 on v0

v1 whole, which is shorter than its diff:
```python
import functools

import jax
import jax.numpy as jnp
from jax import lax
from jax.experimental import pallas as pl
from jax.experimental.pallas import tpu as pltpu
from jax.sharding import PartitionSpec as P


CHUNKS = 8


def turning_kernel(*refs):
    pairs = len(refs) // 7
    sources, terms, scratch = refs[: 2 * pairs], refs[2 * pairs : 3 * pairs], refs[3 * pairs :]
    jobs = []
    for p in range(pairs):
        tokens_hbm, basis_hbm = sources[2 * p : 2 * p + 2]
        tokens, basis, token_sem, basis_sems = scratch[4 * p : 4 * p + 4]
        count, rows, _ = basis.shape
        loads = [pltpu.make_async_copy(tokens_hbm, tokens, token_sem)]
        for k in range(count):
            loads.append(
                pltpu.make_async_copy(
                    basis_hbm.at[pl.ds(k * rows, rows)], basis.at[k], basis_sems.at[k]
                )
            )
        jobs.append(loads)
    for p, loads in enumerate(jobs):
        for k, load in enumerate(loads):
            load.start(priority=int(p > 0) if pairs > 1 else int(2 * k > len(loads)))
    for p, loads in enumerate(jobs):
        tokens, basis = scratch[4 * p : 4 * p + 2]
        count, rows, _ = basis.shape
        loads[0].wait()
        total = None
        for k in range(count):
            loads[k + 1].wait()
            part = jnp.dot(
                tokens[:, k * rows : (k + 1) * rows], basis[k], preferred_element_type=jnp.float32
            )
            total = part if total is None else total + part
        terms[p][...] = total


def turned_terms(*pairs):
    shapes, operands, scratch = [], [], []
    flops = moved = 0
    for tokens, basis in pairs:
        seqs, slots, features = tokens.shape
        dirs = basis.shape[1]
        count = CHUNKS if features % (CHUNKS * 128) == 0 else 1
        rows = seqs * slots
        operands += [tokens.reshape(rows, features), basis]
        shapes.append(pltpu.VMEM((rows, dirs), jnp.float32))
        scratch += [
            pltpu.VMEM((rows, features), tokens.dtype),
            pltpu.VMEM((count, features // count, dirs), basis.dtype),
            pltpu.SemaphoreType.DMA,
            pltpu.SemaphoreType.DMA((count,)),
        ]
        flops += 2 * rows * features * dirs
        moved += 2 * features * (dirs + rows)
    terms = pl.pallas_call(
        turning_kernel,
        out_shape=shapes,
        in_specs=[pl.BlockSpec(memory_space=pltpu.HBM)] * len(operands),
        out_specs=[pl.BlockSpec(memory_space=pltpu.VMEM)] * len(pairs),
        scratch_shapes=scratch,
        cost_estimate=pl.CostEstimate(flops=flops, bytes_accessed=moved, transcendentals=0),
        name="turning",
    )(*operands)
    return [
        term.reshape(tokens.shape[:2] + term.shape[1:]) for term, (tokens, _) in zip(terms, pairs)
    ]


def paired(size):
    return size & (size - 1) == 0


def source(size, own, step):
    return own ^ step if paired(size) else (own - step) % size


def target(size, own, step):
    return own ^ step if paired(size) else (own + step) % size


def sent(value, axis, step):
    size = lax.axis_size(axis)
    return lax.ppermute(value, axis, [(i, target(size, i, step)) for i in range(size)])


def every_token(turned, axis):
    pieces = [turned]
    for k in range(1, lax.axis_size(axis)):
        pieces.append(sent(turned, axis, k))
    return pieces


def summed_part(terms, axis):
    size = lax.axis_size(axis)
    own = lax.axis_index(axis)
    width = terms.shape[2] // size

    def part(owner):
        return lax.dynamic_slice_in_dim(terms, owner * width, width, 2)

    total = part(own)
    for k in range(1, size):
        total = total + sent(part(target(size, own, k)), axis, k)
    return total


def summed_whole(terms, axis):
    if lax.axis_size(axis) > 2:
        return lax.psum(terms, axis)
    return terms + sent(terms, axis, 1)


def tile_kernel(*refs, outs, ins, divisor):
    out_pieces, in_pieces = refs[:outs], refs[outs : outs + ins]
    tile_hbm, kept, turned, tile, sems = refs[outs + ins :]
    for axis, pieces, whole in (("col", out_pieces, kept), ("row", in_pieces, turned)):
        own = lax.axis_index(axis)
        for k, piece in enumerate(pieces):
            slots = piece.shape[1]
            place = pl.multiple_of(source(len(pieces), own, k) * slots, slots)
            whole[:, pl.ds(place, slots), :] = piece[...]
    steps, rows, _ = tile.shape
    writes = []
    for step in range(steps):
        total = None
        for n in range(kept.shape[0]):
            product = lax.dot_general(
                kept[n, :, step * rows : (step + 1) * rows],
                turned[n],
                (((0,), (0,)), ((), ())),
                preferred_element_type=jnp.float32,
            )
            square = product * product
            total = square if total is None else total + square
        tile[step] = total * (1.0 / divisor) if paired(divisor) else total / divisor
        write = pltpu.make_async_copy(
            tile.at[step], tile_hbm.at[pl.ds(step * rows, rows)], sems.at[step]
        )
        write.start()
        writes.append(write)
    for write in writes:
        write.wait()


def tile_of(out_pieces, in_pieces):
    seqs, out_slots, rows = out_pieces[0].shape
    cols = in_pieces[0].shape[2]
    slot_total = out_slots * len(out_pieces)
    steps = 4 if rows % 512 == 0 else 1
    dtype = out_pieces[0].dtype
    pieces = [
        pltpu.with_memory_space_constraint(piece, pltpu.VMEM) for piece in out_pieces + in_pieces
    ]
    return pl.pallas_call(
        functools.partial(
            tile_kernel, outs=len(out_pieces), ins=len(in_pieces), divisor=seqs * slot_total
        ),
        out_shape=jax.ShapeDtypeStruct((rows, cols), jnp.float32),
        in_specs=[pl.BlockSpec(memory_space=pltpu.VMEM)] * len(pieces),
        out_specs=pl.BlockSpec(memory_space=pltpu.HBM),
        scratch_shapes=[
            pltpu.VMEM((seqs, slot_total, rows), dtype),
            pltpu.VMEM((seqs, slot_total, cols), dtype),
            pltpu.VMEM((steps, rows // steps, cols), jnp.float32),
            pltpu.SemaphoreType.DMA((steps,)),
        ],
        cost_estimate=pl.CostEstimate(
            flops=2 * seqs * slot_total * rows * cols,
            bytes_accessed=4 * rows * cols,
            transcendentals=0,
        ),
        name="tile",
    )(*pieces)


def local(activations, gradients, basis_in, basis_out, lengths):
    slots = gradients.shape[1]
    out_terms, in_terms = turned_terms((gradients, basis_out), (activations, basis_in))
    turned_out = summed_part(out_terms, "seq").astype(jnp.bfloat16)
    turned_in = summed_whole(in_terms, "seq").astype(jnp.bfloat16)
    token = lax.axis_index("col") * slots + jnp.arange(slots)
    live = token[None, :] < lengths[:, None]
    kept = jnp.where(live[:, :, None], turned_out, jnp.zeros((), jnp.bfloat16))
    return tile_of(every_token(kept, "col"), every_token(turned_in, "row"))


def solution(mesh):
    return jax.shard_map(
        local,
        mesh=mesh,
        in_specs=(
            P(None, "row", "seq"),
            P(None, "col", "seq"),
            P("seq", "col"),
            P("seq", "row"),
            P(),
        ),
        out_specs=P(("row", "seq"), "col"),
        check_vma=False,
    )
```

time: 118 us -> 26.6 us (0.23)
  waiting for transfers between devices: 67.3 us -> 4.84 us
  blocking collectives: 18.8 us -> 0 us
  matrix products: 13.9 us -> 0 us
  between operations: 13.1 us -> 0.04 us
  starting transfers between devices: 0.09 us -> 12.2 us
  Pallas kernels: 0 us -> 9.21 us
  other arithmetic: 2.38 us -> 0.17 us
  local copies, waits for them, and re-layouts: 1.62 us -> 0.02 us
    reduce_scatter x3 -> x0, waiting for transfers between devices: 67.2 us -> none  [the longest x1 54.7 us: local(): return lax.psum_scatter(squared, 'seq', scatter_dimension=0, tiled=True)]
    all_gather x2 -> x0, blocking collectives: 18.8 us -> none  [the longest x1 13.4 us: local(): every_out = lax.all_gather(turned_out, 'col', axis=0, tiled=True)]
    dot_general x3 -> x0, matrix products: 13.9 us -> none  [the longest x2 11.2 us: turned_terms(): jnp.einsum('ntf,fk->ntk', tokens, basis, preferred_element_type=jnp.float32)]
    ppermute x0 -> x8, starting transfers between devices: none -> 12.2 us  [sent(): lax.ppermute(value, axis, [(i, target(size, i, step)) for i in range(size)])]
    pallas_call x0 -> x2, Pallas kernels: none -> 9.21 us  [the longest x1 7.52 us: turned_terms(): pl.pallas_call(turning_kernel, out_shape=shapes, in_specs=[pl.BlockSpec(m...]
    ppermute x0 -> x8, waiting for transfers between devices: none -> 4.84 us  [sent(): lax.ppermute(value, axis, [(i, target(size, i, step)) for i in range(size)])]
    convert_element_type x2 -> x1, other arithmetic: 1.69 us -> 0.02 us  [local(): turned_in = summed_whole(in_terms, 'seq').astype(jnp.bfloat16)]
  transfers between devices with their start and end apart: 3 -> 8, of which waited for: 3 -> 3; matrix products, arithmetic and copies ran while one was open for 7% -> 1% of each run, Pallas kernels for 0% -> 0%
where the time goes in v1:
time: 26.6 us; the launch traced here: 26.5 us
  starting transfers between devices  12.2 us (46%)
  Pallas kernels  9.21 us (35%)
  waiting for transfers between devices  4.84 us (18%)
    ppermute x8, starting transfers between devices, sent(): lax.ppermute(value, axis, [(i, target(size, i, step)) for i in range(size)])  12.2 us
    pallas_call x1, Pallas kernels, turned_terms(): pl.pallas_call(turning_kernel, out_shape=shapes, in_specs=[pl.BlockSpec(m...  7.52 us
    ppermute x8, waiting for transfers between devices, sent(): lax.ppermute(value, axis, [(i, target(size, i, step)) for i in range(size)])  4.84 us
    pallas_call x1, Pallas kernels, tile_of(): pl.pallas_call(functools.partial(tile_kernel, outs=len(out_pieces), ins=l...  1.69 us
  transfers between devices with their start and end apart: 8, of which 3 were waited for; matrix products, arithmetic and copies ran while one was open for 1% of the time, Pallas kernels for 0%

profile of v1, /device:TPU:0, one launch (start us, length us, event | category | flops | bytes accessed | tf_op | source)
XLA Modules:
  0.0 26.5 jit_solution(7223071667086046682)
XLA Ops:
  0.0 0.0 copy-start
  0.0 7.5 %turning.1 = (f32[32,1024]{1,0:T(8,128)S(1)}, f32[32,1024]{1,0:T(8,128)S(1)}) custom-call(bf16[32,4096]{1,0:T(8,128)(2,1)} %bitcast.8, bf16[4096,1024]{1,0:T(8,128)(2,1)} %refs_1_.1, bf16[32,4096]{1,0:T(8,128)(2,1)} %bitcast.9, bf16[4096,1024]{1,0:T(8,128)(2,1)} %refs_3_.1), custom_call_target="tpu_custom_call" | custom-call | flops 536870912 | bytes 17301504 | tf_op jit(solution)/shard_map/turning/pallas_call | solution.py:65
  7.5 3.0 %collective-permute-start = (f32[2,16,512]{2,1,0:T(8,128)S(1)}, f32[2,16,512]{2,1,0:T(8,128)S(1)}, u32[]{:S(2)}, u32[]{:S(2)}) collective-permute-start(f32[2,16,512]{2,1,0:T(8,128)S(1)} %constant_dynamic-slice_fusion), channel_id=1, source_target_pairs={{0,16},{16,0},{1,17},{17,1},{2,18},{18,2},{3,19},{19,3},{4,20},{20... | collective-permute-start | bytes 196616 | tf_op jit(solution)/shard_map/ppermute | solution.py:93
  10.6 0.1 collective-permute-start.4
  10.7 0.0 copy-done
  10.7 0.1 broadcast_compare_fusion
  10.7 2.3 %collective-permute-done = f32[2,16,512]{2,1,0:T(8,128)S(1)} collective-permute-done((f32[2,16,512]{2,1,0:T(8,128)S(1)}, f32[2,16,512]{2,1,0:T(8,128)S(1)}, u32[]{:S(2)}, u32[]{:S(2)}) %collective-permute-start) | collective-permute-done | bytes 65568 | tf_op jit(solution)/shard_map/ppermute | solution.py:93
  13.1 0.1 fusion.refs_0_
  13.1 4.5 %collective-permute-start.3 = (bf16[2,16,512]{2,1,0:T(8,128)(2,1)S(1)}, bf16[2,16,512]{2,1,0:T(8,128)(2,1)S(1)}, u32[]{:S(2)}, u32[]{:S(2)}) collective-permute-start(bf16[2,16,512]{2,1,0:T(8,128)(2,1)S(1)} %fusion.refs_0_), channel_id=1, source_target_pairs={{0,3},{1,2},{2,1},{3,0},{4,7},{5,6},{6,5},{7,4},{8,11},{9,10},{10,... | collective-permute-start | bytes 98312 | tf_op jit(solution)/shard_map/ppermute | solution.py:93
  17.7 0.0 collective-permute-done.4
  17.7 0.1 collective-permute-start.7
  17.8 1.6 %collective-permute-start.6 = (bf16[2,16,1024]{2,1,0:T(8,128)(2,1)S(1)}, bf16[2,16,1024]{2,1,0:T(8,128)(2,1)S(1)}, u32[]{:S(2)}, u32[]{:S(2)}) collective-permute-start(bf16[2,16,1024]{2,1,0:T(8,128)(2,1)S(1)} %add_convert_fusion.refs_4_), channel_id=1, source_target_pairs={{0,8},{4,12},{8,0},{12,4},{1,9},{5,13},{9,1},{13,5},{2,10},{6,14},... | collective-permute-start | bytes 196616 | tf_op jit(solution)/shard_map/ppermute | solution.py:93
  19.4 0.3 collective-permute-start.5
  19.6 1.1 %collective-permute-start.2 = (bf16[2,16,512]{2,1,0:T(8,128)(2,1)S(1)}, bf16[2,16,512]{2,1,0:T(8,128)(2,1)S(1)}, u32[]{:S(2)}, u32[]{:S(2)}) collective-permute-start(bf16[2,16,512]{2,1,0:T(8,128)(2,1)S(1)} %fusion.refs_0_), channel_id=1, source_target_pairs={{0,2},{1,3},{2,0},{3,1},{4,6},{5,7},{6,4},{7,5},{8,10},{9,11},{10,... | collective-permute-start | bytes 98312 | tf_op jit(solution)/shard_map/ppermute | solution.py:93
  20.7 0.0 collective-permute-done.3.refs_3_
  20.7 1.6 %collective-permute-start.1 = (bf16[2,16,512]{2,1,0:T(8,128)(2,1)S(1)}, bf16[2,16,512]{2,1,0:T(8,128)(2,1)S(1)}, u32[]{:S(2)}, u32[]{:S(2)}) collective-permute-start(bf16[2,16,512]{2,1,0:T(8,128)(2,1)S(1)} %fusion.refs_0_), channel_id=1, source_target_pairs={{0,1},{1,0},{2,3},{3,2},{4,5},{5,4},{6,7},{7,6},{8,9},{9,8},{10,11... | collective-permute-start | bytes 98312 | tf_op jit(solution)/shard_map/ppermute | solution.py:93
  22.3 2.1 %collective-permute-done.2.refs_2_ = bf16[2,16,512]{2,1,0:T(8,128)(2,1)S(1)} collective-permute-done((bf16[2,16,512]{2,1,0:T(8,128)(2,1)S(1)}, bf16[2,16,512]{2,1,0:T(8,128)(2,1)S(1)}, u32[]{:S(2)}, u32[]{:S(2)}) %collective-permute-start.2) | collective-permute-done | bytes 32800 | tf_op jit(solution)/shard_map/ppermute | solution.py:93
  24.4 0.4 %collective-permute-done.1.refs_1_ = bf16[2,16,512]{2,1,0:T(8,128)(2,1)S(1)} collective-permute-done((bf16[2,16,512]{2,1,0:T(8,128)(2,1)S(1)}, bf16[2,16,512]{2,1,0:T(8,128)(2,1)S(1)}, u32[]{:S(2)}, u32[]{:S(2)}) %collective-permute-start.1) | collective-permute-done | bytes 32800 | tf_op jit(solution)/shard_map/ppermute | solution.py:93
  24.8 0.0 collective-permute-done.7.refs_7_
  24.8 0.0 collective-permute-done.6.refs_6_
  24.8 0.0 collective-permute-done.5.refs_5_
  24.8 1.7 %tile.1 = f32[512,1024]{1,0:T(8,128)} custom-call(bf16[2,16,512]{2,1,0:T(8,128)(2,1)S(1)} %fusion.refs_0_, bf16[2,16,512]{2,1,0:T(8,128)(2,1)S(1)} %collective-permute-done.1.refs_1_, bf16[2,16,512]{2,1,0:T(8,128)(2,1)S(1)} %collective-permute-done.2.refs_2_, bf16[2,16,512]{2,1,0:T(8,128)(2,1)S(1)} %collective-permute-done.3.refs_3_, ...), custom_call_target="tpu_custom_call" | custom-call | flops 134217728 | bytes 2097152 | tf_op jit(solution)/shard_map/tile/pallas_call | solution.py:164
  (3 shorter events, 0.0 us)
Async XLA Ops:
  0.0 10.7 %copy-start = (s32[2]{0:T(128)S(1)}, s32[2]{0:T(128)}, u32[]{:S(2)}) copy-start(s32[2]{0:T(128)} %param.9) | copy-start | bytes 28
  7.5 5.5 %collective-permute-start = (f32[2,16,512]{2,1,0:T(8,128)S(1)}, f32[2,16,512]{2,1,0:T(8,128)S(1)}, u32[]{:S(2)}, u32[]{:S(2)}) collective-permute-start(f32[2,16,512]{2,1,0:T(8,128)S(1)} %constant_dynamic-slice_fusion), channel_id=1, source_target_pairs={{0,16},{16,0},{1,17},{17,1},{2,18},{18,2},{3,19},{19,3},{4,20},{20... | collective-permute-start | bytes 196616 | tf_op jit(solution)/shard_map/ppermute | solution.py:93
  10.6 7.1 %collective-permute-start.4 = (f32[2,16,1024]{2,1,0:T(8,128)S(1)}, f32[2,16,1024]{2,1,0:T(8,128)S(1)}, u32[]{:S(2)}, u32[]{:S(2)}) collective-permute-start(f32[2,16,1024]{2,1,0:T(8,128)S(1)} %bitcast.4), channel_id=1, source_target_pairs={{0,16},{16,0},{1,17},{17,1},{2,18},{18,2},{3,19},{19,3},{4,20},{20... | collective-permute-start | bytes 393224 | tf_op jit(solution)/shard_map/ppermute | solution.py:93
  13.1 7.6 %collective-permute-start.3 = (bf16[2,16,512]{2,1,0:T(8,128)(2,1)S(1)}, bf16[2,16,512]{2,1,0:T(8,128)(2,1)S(1)}, u32[]{:S(2)}, u32[]{:S(2)}) collective-permute-start(bf16[2,16,512]{2,1,0:T(8,128)(2,1)S(1)} %fusion.refs_0_), channel_id=1, source_target_pairs={{0,3},{1,2},{2,1},{3,0},{4,7},{5,6},{6,5},{7,4},{8,11},{9,10},{10,... | collective-permute-start | bytes 98312 | tf_op jit(solution)/shard_map/ppermute | solution.py:93
  17.7 7.1 %collective-permute-start.7 = (bf16[2,16,1024]{2,1,0:T(8,128)(2,1)S(1)}, bf16[2,16,1024]{2,1,0:T(8,128)(2,1)S(1)}, u32[]{:S(2)}, u32[]{:S(2)}) collective-permute-start(bf16[2,16,1024]{2,1,0:T(8,128)(2,1)S(1)} %add_convert_fusion.refs_4_), channel_id=1, source_target_pairs={{0,12},{4,8},{8,4},{12,0},{1,13},{5,9},{9,5},{13,1},{2,14},{6,10},... | collective-permute-start | bytes 196616 | tf_op jit(solution)/shard_map/ppermute | solution.py:93
  17.8 7.0 %collective-permute-start.6 = (bf16[2,16,1024]{2,1,0:T(8,128)(2,1)S(1)}, bf16[2,16,1024]{2,1,0:T(8,128)(2,1)S(1)}, u32[]{:S(2)}, u32[]{:S(2)}) collective-permute-start(bf16[2,16,1024]{2,1,0:T(8,128)(2,1)S(1)} %add_convert_fusion.refs_4_), channel_id=1, source_target_pairs={{0,8},{4,12},{8,0},{12,4},{1,9},{5,13},{9,1},{13,5},{2,10},{6,14},... | collective-permute-start | bytes 196616 | tf_op jit(solution)/shard_map/ppermute | solution.py:93
  19.4 5.4 %collective-permute-start.5 = (bf16[2,16,1024]{2,1,0:T(8,128)(2,1)S(1)}, bf16[2,16,1024]{2,1,0:T(8,128)(2,1)S(1)}, u32[]{:S(2)}, u32[]{:S(2)}) collective-permute-start(bf16[2,16,1024]{2,1,0:T(8,128)(2,1)S(1)} %add_convert_fusion.refs_4_), channel_id=1, source_target_pairs={{0,4},{4,0},{8,12},{12,8},{1,5},{5,1},{9,13},{13,9},{2,6},{6,2},{1... | collective-permute-start | bytes 196616 | tf_op jit(solution)/shard_map/ppermute | solution.py:93
  19.6 4.8 %collective-permute-start.2 = (bf16[2,16,512]{2,1,0:T(8,128)(2,1)S(1)}, bf16[2,16,512]{2,1,0:T(8,128)(2,1)S(1)}, u32[]{:S(2)}, u32[]{:S(2)}) collective-permute-start(bf16[2,16,512]{2,1,0:T(8,128)(2,1)S(1)} %fusion.refs_0_), channel_id=1, source_target_pairs={{0,2},{1,3},{2,0},{3,1},{4,6},{5,7},{6,4},{7,5},{8,10},{9,11},{10,... | collective-permute-start | bytes 98312 | tf_op jit(solution)/shard_map/ppermute | solution.py:93
  20.7 4.1 %collective-permute-start.1 = (bf16[2,16,512]{2,1,0:T(8,128)(2,1)S(1)}, bf16[2,16,512]{2,1,0:T(8,128)(2,1)S(1)}, u32[]{:S(2)}, u32[]{:S(2)}) collective-permute-start(bf16[2,16,512]{2,1,0:T(8,128)(2,1)S(1)} %fusion.refs_0_), channel_id=1, source_target_pairs={{0,1},{1,0},{2,3},{3,2},{4,5},{5,4},{6,7},{7,6},{8,9},{9,8},{10,11... | collective-permute-start | bytes 98312 | tf_op jit(solution)/shard_map/ppermute | solution.py:93

commit v2 on v1

--- a/solution.py
+++ b/solution.py
@@ -52,7 +52,10 @@
         dirs = basis.shape[1]
         count = CHUNKS if features % (CHUNKS * 128) == 0 else 1
         rows = seqs * slots
-        operands += [tokens.reshape(rows, features), basis]
+        operands += [
+            pltpu.with_memory_space_constraint(array, pltpu.HBM)
+            for array in (tokens.reshape(rows, features), basis)
+        ]
         shapes.append(pltpu.VMEM((rows, dirs), jnp.float32))
         scratch += [
             pltpu.VMEM((rows, features), tokens.dtype),
@@ -69,11 +72,37 @@
         out_specs=[pl.BlockSpec(memory_space=pltpu.VMEM)] * len(pairs),
         scratch_shapes=scratch,
         cost_estimate=pl.CostEstimate(flops=flops, bytes_accessed=moved, transcendentals=0),
+        compiler_params=pltpu.CompilerParams(vmem_limit_bytes=24 << 20),
         name="turning",
     )(*operands)
     return [
         term.reshape(tokens.shape[:2] + term.shape[1:]) for term, (tokens, _) in zip(terms, pairs)
     ]
+
+
+def held_kernel(tokens, basis, terms):
+    terms[...] = jnp.dot(tokens[...], basis[...], preferred_element_type=jnp.float32)
+
+
+def held_terms(tokens, basis):
+    seqs, slots, features = tokens.shape
+    dirs = basis.shape[1]
+    rows = seqs * slots
+    terms = pl.pallas_call(
+        held_kernel,
+        out_shape=pltpu.VMEM((rows, dirs), jnp.float32),
+        in_specs=[pl.BlockSpec(memory_space=pltpu.VMEM)] * 2,
+        out_specs=pl.BlockSpec(memory_space=pltpu.VMEM),
+        cost_estimate=pl.CostEstimate(
+            flops=2 * rows * features * dirs, bytes_accessed=4 * rows * dirs, transcendentals=0
+        ),
+        compiler_params=pltpu.CompilerParams(vmem_limit_bytes=24 << 20),
+        name="held",
+    )(
+        pltpu.with_memory_space_constraint(tokens.reshape(rows, features), pltpu.VMEM),
+        pltpu.with_memory_space_constraint(basis, pltpu.VMEM),
+    )
+    return terms.reshape(seqs, slots, dirs)
 
 
 def paired(size):
@@ -185,7 +214,8 @@
 
 def local(activations, gradients, basis_in, basis_out, lengths):
     slots = gradients.shape[1]
-    out_terms, in_terms = turned_terms((gradients, basis_out), (activations, basis_in))
+    (out_terms,) = turned_terms((gradients, basis_out))
+    in_terms = held_terms(activations, basis_in)
     turned_out = summed_part(out_terms, "seq").astype(jnp.bfloat16)
     turned_in = summed_whole(in_terms, "seq").astype(jnp.bfloat16)
     token = lax.axis_index("col") * slots + jnp.arange(slots)

time: 26.6 us -> 24.7 us (0.929)
  waiting for transfers between devices: 4.84 us -> 2.35 us
  starting transfers between devices: 12.2 us -> 14.6 us
  Pallas kernels: 9.21 us -> 7.36 us
    pallas_call x1, Pallas kernels: 7.52 us -> 4.11 us  [turned_terms(): pl.pallas_call(turning_kernel, out_shape=shapes, in_specs=[pl.BlockSpec(m...]
    ppermute x8, waiting for transfers between devices: 4.84 us -> 2.35 us  [sent(): lax.ppermute(value, axis, [(i, target(size, i, step)) for i in range(size)])]
    ppermute x8, starting transfers between devices: 12.2 us -> 14.6 us  [sent(): lax.ppermute(value, axis, [(i, target(size, i, step)) for i in range(size)])]
    pallas_call x0 -> x1, Pallas kernels: none -> 1.54 us  [held_terms(): pl.pallas_call(held_kernel, out_shape=pltpu.VMEM((rows, dirs), jnp.float3...]
  transfers between devices with their start and end apart: 8 -> 8, of which waited for: 3 -> 2; matrix products, arithmetic and copies ran while one was open for 1% -> 1% of each run, Pallas kernels for 0% -> 6%
where the time goes in v2:
time: 24.7 us; the launch traced here: 24.5 us
  starting transfers between devices  14.6 us (59%)
  Pallas kernels  7.36 us (30%)
  waiting for transfers between devices  2.35 us (10%)
    ppermute x8, starting transfers between devices, sent(): lax.ppermute(value, axis, [(i, target(size, i, step)) for i in range(size)])  14.6 us
    pallas_call x1, Pallas kernels, turned_terms(): pl.pallas_call(turning_kernel, out_shape=shapes, in_specs=[pl.BlockSpec(m...  4.11 us
    ppermute x8, waiting for transfers between devices, sent(): lax.ppermute(value, axis, [(i, target(size, i, step)) for i in range(size)])  2.35 us
    pallas_call x1, Pallas kernels, tile_of(): pl.pallas_call(functools.partial(tile_kernel, outs=len(out_pieces), ins=l...  1.72 us
    pallas_call x1, Pallas kernels, held_terms(): pl.pallas_call(held_kernel, out_shape=pltpu.VMEM((rows, dirs), jnp.float3...  1.54 us
  transfers between devices with their start and end apart: 8, of which 2 were waited for; matrix products, arithmetic and copies ran while one was open for 1% of the time, Pallas kernels for 6%

profile of v2, /device:TPU:0, one launch (start us, length us, event | category | flops | bytes accessed | tf_op | source)
XLA Modules:
  0.0 24.5 jit_solution(3275173029004644703)
XLA Ops:
  0.0 0.0 copy-start.1
  0.0 0.0 copy-start
  0.0 0.0 copy-start.2
  0.0 4.1 %turning.1 = f32[32,1024]{1,0:T(8,128)S(1)} custom-call(bf16[32,4096]{1,0:T(8,128)(2,1)} %bitcast.9, bf16[4096,1024]{1,0:T(8,128)(2,1)} %refs_1_.1), custom_call_target="tpu_custom_call" | custom-call | flops 268435456 | bytes 8650752 | tf_op jit(solution)/shard_map/turning/pallas_call | solution.py:68
  4.1 3.0 %collective-permute-start = (f32[2,16,512]{2,1,0:T(8,128)S(1)}, f32[2,16,512]{2,1,0:T(8,128)S(1)}, u32[]{:S(2)}, u32[]{:S(2)}) collective-permute-start(f32[2,16,512]{2,1,0:T(8,128)S(1)} %constant_dynamic-slice_fusion), channel_id=1, source_target_pairs={{0,16},{16,0},{1,17},{17,1},{2,18},{18,2},{3,19},{19,3},{4,20},{20... | collective-permute-start | bytes 196616 | tf_op jit(solution)/shard_map/ppermute | solution.py:122
  7.2 0.0 copy-done.1
  7.2 0.0 copy-done
  7.2 1.5 %held.1 = f32[32,1024]{1,0:T(8,128)S(1)} custom-call(bf16[32,4096]{1,0:T(8,128)(2,1)S(1)} %bitcast.8, bf16[4096,1024]{1,0:T(8,128)(2,1)S(1)} %copy-done), custom_call_target="tpu_custom_call" | custom-call | flops 268435456 | bytes 131072 | tf_op jit(solution)/shard_map/held/pallas_call | solution.py:91
  8.7 1.9 %collective-permute-start.4 = (f32[2,16,1024]{2,1,0:T(8,128)S(1)}, f32[2,16,1024]{2,1,0:T(8,128)S(1)}, u32[]{:S(2)}, u32[]{:S(2)}) collective-permute-start(f32[2,16,1024]{2,1,0:T(8,128)S(1)} %bitcast.4), channel_id=1, source_target_pairs={{0,16},{16,0},{1,17},{17,1},{2,18},{18,2},{3,19},{19,3},{4,20},{20... | collective-permute-start | bytes 393224 | tf_op jit(solution)/shard_map/ppermute | solution.py:122
  10.6 0.0 copy-done.2
  10.6 0.1 broadcast_compare_fusion
  10.7 0.0 collective-permute-done
  10.7 0.1 fusion.refs_0_
  10.8 3.6 %collective-permute-start.3 = (bf16[2,16,512]{2,1,0:T(8,128)(2,1)S(1)}, bf16[2,16,512]{2,1,0:T(8,128)(2,1)S(1)}, u32[]{:S(2)}, u32[]{:S(2)}) collective-permute-start(bf16[2,16,512]{2,1,0:T(8,128)(2,1)S(1)} %fusion.refs_0_), channel_id=1, source_target_pairs={{0,3},{1,2},{2,1},{3,0},{4,7},{5,6},{6,5},{7,4},{8,11},{9,10},{10,... | collective-permute-start | bytes 98312 | tf_op jit(solution)/shard_map/ppermute | solution.py:122
  14.4 0.0 collective-permute-done.4
  14.4 0.5 %collective-permute-start.7 = (bf16[2,16,1024]{2,1,0:T(8,128)(2,1)S(1)}, bf16[2,16,1024]{2,1,0:T(8,128)(2,1)S(1)}, u32[]{:S(2)}, u32[]{:S(2)}) collective-permute-start(bf16[2,16,1024]{2,1,0:T(8,128)(2,1)S(1)} %add_convert_fusion.refs_4_), channel_id=1, source_target_pairs={{0,12},{4,8},{8,4},{12,0},{1,13},{5,9},{9,5},{13,1},{2,14},{6,10},... | collective-permute-start | bytes 196616 | tf_op jit(solution)/shard_map/ppermute | solution.py:122
  14.9 1.2 %collective-permute-start.6 = (bf16[2,16,1024]{2,1,0:T(8,128)(2,1)S(1)}, bf16[2,16,1024]{2,1,0:T(8,128)(2,1)S(1)}, u32[]{:S(2)}, u32[]{:S(2)}) collective-permute-start(bf16[2,16,1024]{2,1,0:T(8,128)(2,1)S(1)} %add_convert_fusion.refs_4_), channel_id=1, source_target_pairs={{0,8},{4,12},{8,0},{12,4},{1,9},{5,13},{9,1},{13,5},{2,10},{6,14},... | collective-permute-start | bytes 196616 | tf_op jit(solution)/shard_map/ppermute | solution.py:122
  16.1 0.3 %collective-permute-start.5 = (bf16[2,16,1024]{2,1,0:T(8,128)(2,1)S(1)}, bf16[2,16,1024]{2,1,0:T(8,128)(2,1)S(1)}, u32[]{:S(2)}, u32[]{:S(2)}) collective-permute-start(bf16[2,16,1024]{2,1,0:T(8,128)(2,1)S(1)} %add_convert_fusion.refs_4_), channel_id=1, source_target_pairs={{0,4},{4,0},{8,12},{12,8},{1,5},{5,1},{9,13},{13,9},{2,6},{6,2},{1... | collective-permute-start | bytes 196616 | tf_op jit(solution)/shard_map/ppermute | solution.py:122
  16.3 2.6 %collective-permute-start.2 = (bf16[2,16,512]{2,1,0:T(8,128)(2,1)S(1)}, bf16[2,16,512]{2,1,0:T(8,128)(2,1)S(1)}, u32[]{:S(2)}, u32[]{:S(2)}) collective-permute-start(bf16[2,16,512]{2,1,0:T(8,128)(2,1)S(1)} %fusion.refs_0_), channel_id=1, source_target_pairs={{0,2},{1,3},{2,0},{3,1},{4,6},{5,7},{6,4},{7,5},{8,10},{9,11},{10,... | collective-permute-start | bytes 98312 | tf_op jit(solution)/shard_map/ppermute | solution.py:122
  18.9 0.0 collective-permute-done.3.refs_3_
  18.9 1.6 %collective-permute-start.1 = (bf16[2,16,512]{2,1,0:T(8,128)(2,1)S(1)}, bf16[2,16,512]{2,1,0:T(8,128)(2,1)S(1)}, u32[]{:S(2)}, u32[]{:S(2)}) collective-permute-start(bf16[2,16,512]{2,1,0:T(8,128)(2,1)S(1)} %fusion.refs_0_), channel_id=1, source_target_pairs={{0,1},{1,0},{2,3},{3,2},{4,5},{5,4},{6,7},{7,6},{8,9},{9,8},{10,11... | collective-permute-start | bytes 98312 | tf_op jit(solution)/shard_map/ppermute | solution.py:122
  20.5 0.7 %collective-permute-done.2.refs_2_ = bf16[2,16,512]{2,1,0:T(8,128)(2,1)S(1)} collective-permute-done((bf16[2,16,512]{2,1,0:T(8,128)(2,1)S(1)}, bf16[2,16,512]{2,1,0:T(8,128)(2,1)S(1)}, u32[]{:S(2)}, u32[]{:S(2)}) %collective-permute-start.2) | collective-permute-done | bytes 32800 | tf_op jit(solution)/shard_map/ppermute | solution.py:122
  21.1 1.7 %collective-permute-done.1.refs_1_ = bf16[2,16,512]{2,1,0:T(8,128)(2,1)S(1)} collective-permute-done((bf16[2,16,512]{2,1,0:T(8,128)(2,1)S(1)}, bf16[2,16,512]{2,1,0:T(8,128)(2,1)S(1)}, u32[]{:S(2)}, u32[]{:S(2)}) %collective-permute-start.1) | collective-permute-done | bytes 32800 | tf_op jit(solution)/shard_map/ppermute | solution.py:122
  22.8 0.0 collective-permute-done.7.refs_7_
  22.8 0.0 collective-permute-done.6.refs_6_
  22.8 0.0 collective-permute-done.5.refs_5_
  22.8 1.7 %tile.1 = f32[512,1024]{1,0:T(8,128)} custom-call(bf16[2,16,512]{2,1,0:T(8,128)(2,1)S(1)} %fusion.refs_0_, bf16[2,16,512]{2,1,0:T(8,128)(2,1)S(1)} %collective-permute-done.1.refs_1_, bf16[2,16,512]{2,1,0:T(8,128)(2,1)S(1)} %collective-permute-done.2.refs_2_, bf16[2,16,512]{2,1,0:T(8,128)(2,1)S(1)} %collective-permute-done.3.refs_3_, ...), custom_call_target="tpu_custom_call" | custom-call | flops 134217728 | bytes 2097152 | tf_op jit(solution)/shard_map/tile/pallas_call | solution.py:193
  (3 shorter events, 0.0 us)
Async XLA Ops:
  0.0 7.2 %copy-start.1 = (bf16[2,16,4096]{2,1,0:T(8,128)(2,1)S(1)}, bf16[2,16,4096]{2,1,0:T(8,128)(2,1)}, u32[]{:S(2)}) copy-start(bf16[2,16,4096]{2,1,0:T(8,128)(2,1)} %param.5) | copy-start | bytes 786436
  0.0 7.2 %copy-start = (bf16[4096,1024]{1,0:T(8,128)(2,1)S(1)}, bf16[4096,1024]{1,0:T(8,128)(2,1)}, u32[]{:S(2)}) copy-start(bf16[4096,1024]{1,0:T(8,128)(2,1)} %basis.1) | copy-start | bytes 25165828
  0.0 10.6 %copy-start.2 = (s32[2]{0:T(128)S(1)}, s32[2]{0:T(128)}, u32[]{:S(2)}) copy-start(s32[2]{0:T(128)} %param.9) | copy-start | bytes 28
  4.1 6.5 %collective-permute-start = (f32[2,16,512]{2,1,0:T(8,128)S(1)}, f32[2,16,512]{2,1,0:T(8,128)S(1)}, u32[]{:S(2)}, u32[]{:S(2)}) collective-permute-start(f32[2,16,512]{2,1,0:T(8,128)S(1)} %constant_dynamic-slice_fusion), channel_id=1, source_target_pairs={{0,16},{16,0},{1,17},{17,1},{2,18},{18,2},{3,19},{19,3},{4,20},{20... | collective-permute-start | bytes 196616 | tf_op jit(solution)/shard_map/ppermute | solution.py:122
  8.7 5.7 %collective-permute-start.4 = (f32[2,16,1024]{2,1,0:T(8,128)S(1)}, f32[2,16,1024]{2,1,0:T(8,128)S(1)}, u32[]{:S(2)}, u32[]{:S(2)}) collective-permute-start(f32[2,16,1024]{2,1,0:T(8,128)S(1)} %bitcast.4), channel_id=1, source_target_pairs={{0,16},{16,0},{1,17},{17,1},{2,18},{18,2},{3,19},{19,3},{4,20},{20... | collective-permute-start | bytes 393224 | tf_op jit(solution)/shard_map/ppermute | solution.py:122
  10.8 8.1 %collective-permute-start.3 = (bf16[2,16,512]{2,1,0:T(8,128)(2,1)S(1)}, bf16[2,16,512]{2,1,0:T(8,128)(2,1)S(1)}, u32[]{:S(2)}, u32[]{:S(2)}) collective-permute-start(bf16[2,16,512]{2,1,0:T(8,128)(2,1)S(1)} %fusion.refs_0_), channel_id=1, source_target_pairs={{0,3},{1,2},{2,1},{3,0},{4,7},{5,6},{6,5},{7,4},{8,11},{9,10},{10,... | collective-permute-start | bytes 98312 | tf_op jit(solution)/shard_map/ppermute | solution.py:122
  14.4 8.4 %collective-permute-start.7 = (bf16[2,16,1024]{2,1,0:T(8,128)(2,1)S(1)}, bf16[2,16,1024]{2,1,0:T(8,128)(2,1)S(1)}, u32[]{:S(2)}, u32[]{:S(2)}) collective-permute-start(bf16[2,16,1024]{2,1,0:T(8,128)(2,1)S(1)} %add_convert_fusion.refs_4_), channel_id=1, source_target_pairs={{0,12},{4,8},{8,4},{12,0},{1,13},{5,9},{9,5},{13,1},{2,14},{6,10},... | collective-permute-start | bytes 196616 | tf_op jit(solution)/shard_map/ppermute | solution.py:122
  14.9 7.9 %collective-permute-start.6 = (bf16[2,16,1024]{2,1,0:T(8,128)(2,1)S(1)}, bf16[2,16,1024]{2,1,0:T(8,128)(2,1)S(1)}, u32[]{:S(2)}, u32[]{:S(2)}) collective-permute-start(bf16[2,16,1024]{2,1,0:T(8,128)(2,1)S(1)} %add_convert_fusion.refs_4_), channel_id=1, source_target_pairs={{0,8},{4,12},{8,0},{12,4},{1,9},{5,13},{9,1},{13,5},{2,10},{6,14},... | collective-permute-start | bytes 196616 | tf_op jit(solution)/shard_map/ppermute | solution.py:122
  16.1 6.8 %collective-permute-start.5 = (bf16[2,16,1024]{2,1,0:T(8,128)(2,1)S(1)}, bf16[2,16,1024]{2,1,0:T(8,128)(2,1)S(1)}, u32[]{:S(2)}, u32[]{:S(2)}) collective-permute-start(bf16[2,16,1024]{2,1,0:T(8,128)(2,1)S(1)} %add_convert_fusion.refs_4_), channel_id=1, source_target_pairs={{0,4},{4,0},{8,12},{12,8},{1,5},{5,1},{9,13},{13,9},{2,6},{6,2},{1... | collective-permute-start | bytes 196616 | tf_op jit(solution)/shard_map/ppermute | solution.py:122
  16.3 4.8 %collective-permute-start.2 = (bf16[2,16,512]{2,1,0:T(8,128)(2,1)S(1)}, bf16[2,16,512]{2,1,0:T(8,128)(2,1)S(1)}, u32[]{:S(2)}, u32[]{:S(2)}) collective-permute-start(bf16[2,16,512]{2,1,0:T(8,128)(2,1)S(1)} %fusion.refs_0_), channel_id=1, source_target_pairs={{0,2},{1,3},{2,0},{3,1},{4,6},{5,7},{6,4},{7,5},{8,10},{9,11},{10,... | collective-permute-start | bytes 98312 | tf_op jit(solution)/shard_map/ppermute | solution.py:122
  18.9 3.9 %collective-permute-start.1 = (bf16[2,16,512]{2,1,0:T(8,128)(2,1)S(1)}, bf16[2,16,512]{2,1,0:T(8,128)(2,1)S(1)}, u32[]{:S(2)}, u32[]{:S(2)}) collective-permute-start(bf16[2,16,512]{2,1,0:T(8,128)(2,1)S(1)} %fusion.refs_0_), channel_id=1, source_target_pairs={{0,1},{1,0},{2,3},{3,2},{4,5},{5,4},{6,7},{7,6},{8,9},{9,8},{10,11... | collective-permute-start | bytes 98312 | tf_op jit(solution)/shard_map/ppermute | solution.py:122

commit v3 on v2

--- a/solution.py
+++ b/solution.py
@@ -8,76 +8,61 @@
 from jax.sharding import PartitionSpec as P
 
 
-CHUNKS = 8
-
-
-def turning_kernel(*refs):
-    pairs = len(refs) // 7
-    sources, terms, scratch = refs[: 2 * pairs], refs[2 * pairs : 3 * pairs], refs[3 * pairs :]
-    jobs = []
-    for p in range(pairs):
-        tokens_hbm, basis_hbm = sources[2 * p : 2 * p + 2]
-        tokens, basis, token_sem, basis_sems = scratch[4 * p : 4 * p + 4]
-        count, rows, _ = basis.shape
-        loads = [pltpu.make_async_copy(tokens_hbm, tokens, token_sem)]
-        for k in range(count):
-            loads.append(
-                pltpu.make_async_copy(
-                    basis_hbm.at[pl.ds(k * rows, rows)], basis.at[k], basis_sems.at[k]
-                )
-            )
-        jobs.append(loads)
-    for p, loads in enumerate(jobs):
-        for k, load in enumerate(loads):
-            load.start(priority=int(p > 0) if pairs > 1 else int(2 * k > len(loads)))
-    for p, loads in enumerate(jobs):
-        tokens, basis = scratch[4 * p : 4 * p + 2]
-        count, rows, _ = basis.shape
-        loads[0].wait()
-        total = None
-        for k in range(count):
-            loads[k + 1].wait()
-            part = jnp.dot(
-                tokens[:, k * rows : (k + 1) * rows], basis[k], preferred_element_type=jnp.float32
-            )
-            total = part if total is None else total + part
-        terms[p][...] = total
-
-
-def turned_terms(*pairs):
-    shapes, operands, scratch = [], [], []
-    flops = moved = 0
-    for tokens, basis in pairs:
-        seqs, slots, features = tokens.shape
-        dirs = basis.shape[1]
-        count = CHUNKS if features % (CHUNKS * 128) == 0 else 1
-        rows = seqs * slots
-        operands += [
-            pltpu.with_memory_space_constraint(array, pltpu.HBM)
-            for array in (tokens.reshape(rows, features), basis)
-        ]
-        shapes.append(pltpu.VMEM((rows, dirs), jnp.float32))
-        scratch += [
+CHUNKS = (2, 2, 2, 1, 1, 1, 1, 1, 1, 1, 1, 1, 1)
+AHEAD = 3
+
+
+def turning_kernel(tokens_hbm, basis_hbm, terms, tokens, basis, token_sem, sems, *, spans, ahead):
+    load = pltpu.make_async_copy(tokens_hbm, tokens, token_sem)
+    load.start()
+    chunks = []
+    for k, span in enumerate(spans):
+        rows = pl.ds(sum(spans[:k]), span)
+        chunks.append(pltpu.make_async_copy(basis_hbm.at[rows], basis.at[rows], sems.at[k]))
+        chunks[k].start(priority=int(k >= ahead))
+    load.wait()
+    total = None
+    for k, span in enumerate(spans):
+        chunks[k].wait()
+        first = sum(spans[:k])
+        part = jnp.dot(
+            tokens[:, first : first + span],
+            basis[first : first + span],
+            preferred_element_type=jnp.float32,
+        )
+        total = part if total is None else total + part
+    terms[...] = total
+
+
+def turned_terms(tokens, basis):
+    seqs, slots, features = tokens.shape
+    dirs = basis.shape[1]
+    rows = seqs * slots
+    unit = features // sum(CHUNKS)
+    spans = [unit * c for c in CHUNKS] if unit % 128 == 0 and unit else [features]
+    terms = pl.pallas_call(
+        functools.partial(turning_kernel, spans=spans, ahead=AHEAD),
+        out_shape=pltpu.VMEM((rows, dirs), jnp.float32),
+        in_specs=[pl.BlockSpec(memory_space=pltpu.HBM)] * 2,
+        out_specs=pl.BlockSpec(memory_space=pltpu.VMEM),
+        scratch_shapes=[
             pltpu.VMEM((rows, features), tokens.dtype),
-            pltpu.VMEM((count, features // count, dirs), basis.dtype),
+            pltpu.VMEM((features, dirs), basis.dtype),
             pltpu.SemaphoreType.DMA,
-            pltpu.SemaphoreType.DMA((count,)),
-        ]
-        flops += 2 * rows * features * dirs
-        moved += 2 * features * (dirs + rows)
-    terms = pl.pallas_call(
-        turning_kernel,
-        out_shape=shapes,
-        in_specs=[pl.BlockSpec(memory_space=pltpu.HBM)] * len(operands),
-        out_specs=[pl.BlockSpec(memory_space=pltpu.VMEM)] * len(pairs),
-        scratch_shapes=scratch,
-        cost_estimate=pl.CostEstimate(flops=flops, bytes_accessed=moved, transcendentals=0),
+            pltpu.SemaphoreType.DMA((len(spans),)),
+        ],
+        cost_estimate=pl.CostEstimate(
+            flops=2 * rows * features * dirs,
+            bytes_accessed=2 * features * (dirs + rows),
+            transcendentals=0,
+        ),
         compiler_params=pltpu.CompilerParams(vmem_limit_bytes=24 << 20),
         name="turning",
-    )(*operands)
-    return [
-        term.reshape(tokens.shape[:2] + term.shape[1:]) for term, (tokens, _) in zip(terms, pairs)
-    ]
+    )(
+        pltpu.with_memory_space_constraint(tokens.reshape(rows, features), pltpu.HBM),
+        pltpu.with_memory_space_constraint(basis, pltpu.HBM),
+    )
+    return terms.reshape(seqs, slots, dirs)
 
 
 def held_kernel(tokens, basis, terms):
@@ -126,6 +111,19 @@
     pieces = [turned]
     for k in range(1, lax.axis_size(axis)):
         pieces.append(sent(turned, axis, k))
+    return pieces
+
+
+def every_token_by_pairs(turned, axis):
+    size = lax.axis_size(axis)
+    if size % 2 or not paired(size):
+        return every_token(turned, axis)
+    pieces = []
+    for k in range(0, size, 2):
+        far = turned
+        if k:
+            far = sent(turned, axis, k)
+        pieces += [far, sent(far, axis, 1)]
     return pieces
 
 
@@ -214,14 +212,14 @@
 
 def local(activations, gradients, basis_in, basis_out, lengths):
     slots = gradients.shape[1]
-    (out_terms,) = turned_terms((gradients, basis_out))
+    out_terms = turned_terms(gradients, basis_out)
     in_terms = held_terms(activations, basis_in)
     turned_out = summed_part(out_terms, "seq").astype(jnp.bfloat16)
     turned_in = summed_whole(in_terms, "seq").astype(jnp.bfloat16)
     token = lax.axis_index("col") * slots + jnp.arange(slots)
     live = token[None, :] < lengths[:, None]
     kept = jnp.where(live[:, :, None], turned_out, jnp.zeros((), jnp.bfloat16))
-    return tile_of(every_token(kept, "col"), every_token(turned_in, "row"))
+    return tile_of(every_token(kept, "col"), every_token_by_pairs(turned_in, "row"))
 
 
 def solution(mesh):

time: 24.7 us -> 28 us (1.13)
  starting transfers between devices: 14.6 us -> 9.9 us
  local copies, waits for them, and re-layouts: 0.03 us -> 4.35 us
  waiting for transfers between devices: 2.35 us -> 6.34 us
  Pallas kernels: 7.36 us -> 7.04 us
    ppermute x8, starting transfers between devices: 14.6 us -> 9.9 us  [sent(): lax.ppermute(value, axis, [(i, target(size, i, step)) for i in range(size)])]
    unnamed x6, local copies, waits for them, and re-layouts: 0.01 us -> 4.33 us
    ppermute x8, waiting for transfers between devices: 2.35 us -> 6.34 us  [sent(): lax.ppermute(value, axis, [(i, target(size, i, step)) for i in range(size)])]
    pallas_call x1, Pallas kernels: 4.11 us -> 3.81 us  [turned_terms(): pl.pallas_call(functools.partial(turning_kernel, spans=spans, ahead=AHEAD...]
  transfers between devices with their start and end apart: 8 -> 8, of which waited for: 2 -> 3; matrix products, arithmetic and copies ran while one was open for 1% -> 1% of each run, Pallas kernels for 6% -> 14%
where the time goes in v3:
time: 28 us; the launch traced here: 27.9 us
  starting transfers between devices  9.9 us (35%)
  Pallas kernels  7.04 us (25%)
  waiting for transfers between devices  6.34 us (23%)
  local copies, waits for them, and re-layouts  4.35 us (16%)
    ppermute x8, starting transfers between devices, sent(): lax.ppermute(value, axis, [(i, target(size, i, step)) for i in range(size)])  9.9 us
    ppermute x8, waiting for transfers between devices, sent(): lax.ppermute(value, axis, [(i, target(size, i, step)) for i in range(size)])  6.34 us
    unnamed x6, local copies, waits for them, and re-layouts  4.33 us
    pallas_call x1, Pallas kernels, turned_terms(): pl.pallas_call(functools.partial(turning_kernel, spans=spans, ahead=AHEAD...  3.81 us
    pallas_call x1, Pallas kernels, tile_of(): pl.pallas_call(functools.partial(tile_kernel, outs=len(out_pieces), ins=l...  1.69 us
    pallas_call x1, Pallas kernels, held_terms(): pl.pallas_call(held_kernel, out_shape=pltpu.VMEM((rows, dirs), jnp.float3...  1.54 us
  transfers between devices with their start and end apart: 8, of which 3 were waited for; matrix products, arithmetic and copies ran while one was open for 1% of the time, Pallas kernels for 14%

profile of v3, /device:TPU:0, one launch (start us, length us, event | category | flops | bytes accessed | tf_op | source)
XLA Modules:
  0.0 27.9 jit_solution(3041656704234926117)
XLA Ops:
  0.0 0.0 copy-start
  0.0 3.4 %copy-done = bf16[4096,1024]{1,0:T(8,128)(2,1)S(1)} copy-done((bf16[4096,1024]{1,0:T(8,128)(2,1)S(1)}, bf16[4096,1024]{1,0:T(8,128)(2,1)}, u32[]{:S(2)}) %copy-start) | copy-done | bytes 8388632
  3.4 0.0 copy-start.1
  3.4 0.9 %copy-done.1 = bf16[2,16,4096]{2,1,0:T(8,128)(2,1)S(1)} copy-done((bf16[2,16,4096]{2,1,0:T(8,128)(2,1)S(1)}, bf16[2,16,4096]{2,1,0:T(8,128)(2,1)}, u32[]{:S(2)}) %copy-start.1) | copy-done | bytes 262168
  4.3 0.0 copy-start.2
  4.3 1.5 %held.1 = f32[32,1024]{1,0:T(8,128)S(1)} custom-call(bf16[32,4096]{1,0:T(8,128)(2,1)S(1)} %bitcast.8, bf16[4096,1024]{1,0:T(8,128)(2,1)S(1)} %copy-done), custom_call_target="tpu_custom_call" | custom-call | flops 268435456 | bytes 131072 | tf_op jit(solution)/shard_map/held/pallas_call | solution.py:76
  5.9 3.0 %collective-permute-start.4 = (f32[2,16,1024]{2,1,0:T(8,128)S(1)}, f32[2,16,1024]{2,1,0:T(8,128)S(1)}, u32[]{:S(2)}, u32[]{:S(2)}) collective-permute-start(f32[2,16,1024]{2,1,0:T(8,128)S(1)} %bitcast.6), channel_id=1, source_target_pairs={{0,16},{16,0},{1,17},{17,1},{2,18},{18,2},{3,19},{19,3},{4,20},{20... | collective-permute-start | bytes 393224 | tf_op jit(solution)/shard_map/ppermute | solution.py:107
  8.9 3.8 %turning.1 = f32[32,1024]{1,0:T(8,128)S(1)} custom-call(bf16[32,4096]{1,0:T(8,128)(2,1)} %bitcast.9, bf16[4096,1024]{1,0:T(8,128)(2,1)} %basis_hbm.1), custom_call_target="tpu_custom_call" | custom-call | flops 268435456 | bytes 8650752 | tf_op jit(solution)/shard_map/turning/pallas_call | solution.py:43
  12.7 0.1 collective-permute-start
  12.8 0.0 collective-permute-done.4
  12.8 2.1 %collective-permute-start.6 = (bf16[2,16,1024]{2,1,0:T(8,128)(2,1)S(1)}, bf16[2,16,1024]{2,1,0:T(8,128)(2,1)S(1)}, u32[]{:S(2)}, u32[]{:S(2)}) collective-permute-start(bf16[2,16,1024]{2,1,0:T(8,128)(2,1)S(1)} %add_convert_fusion.refs_4_), channel_id=1, source_target_pairs={{0,8},{4,12},{8,0},{12,4},{1,9},{5,13},{9,1},{13,5},{2,10},{6,14},... | collective-permute-start | bytes 196616 | tf_op jit(solution)/shard_map/ppermute | solution.py:107
  14.9 0.0 copy-done.2
  14.9 0.1 broadcast_compare_fusion
  15.0 0.0 collective-permute-start.5
  15.0 2.2 %collective-permute-done.6.refs_6_ = bf16[2,16,1024]{2,1,0:T(8,128)(2,1)S(1)} collective-permute-done((bf16[2,16,1024]{2,1,0:T(8,128)(2,1)S(1)}, bf16[2,16,1024]{2,1,0:T(8,128)(2,1)S(1)}, u32[]{:S(2)}, u32[]{:S(2)}) %collective-permute-start.6) | collective-permute-done | bytes 65568 | tf_op jit(solution)/shard_map/ppermute | solution.py:107
  17.2 0.0 collective-permute-start.7
  17.2 0.0 collective-permute-done
  17.2 0.1 fusion.refs_0_
  17.2 4.1 %collective-permute-start.3 = (bf16[2,16,512]{2,1,0:T(8,128)(2,1)S(1)}, bf16[2,16,512]{2,1,0:T(8,128)(2,1)S(1)}, u32[]{:S(2)}, u32[]{:S(2)}) collective-permute-start(bf16[2,16,512]{2,1,0:T(8,128)(2,1)S(1)} %fusion.refs_0_), channel_id=1, source_target_pairs={{0,3},{1,2},{2,1},{3,0},{4,7},{5,6},{6,5},{7,4},{8,11},{9,10},{10,... | collective-permute-start | bytes 98312 | tf_op jit(solution)/shard_map/ppermute | solution.py:107
  21.3 0.0 collective-permute-start.2
  21.3 0.6 %collective-permute-start.1 = (bf16[2,16,512]{2,1,0:T(8,128)(2,1)S(1)}, bf16[2,16,512]{2,1,0:T(8,128)(2,1)S(1)}, u32[]{:S(2)}, u32[]{:S(2)}) collective-permute-start(bf16[2,16,512]{2,1,0:T(8,128)(2,1)S(1)} %fusion.refs_0_), channel_id=1, source_target_pairs={{0,1},{1,0},{2,3},{3,2},{4,5},{5,4},{6,7},{7,6},{8,9},{9,8},{10,11... | collective-permute-start | bytes 98312 | tf_op jit(solution)/shard_map/ppermute | solution.py:107
  22.0 1.4 %collective-permute-done.3.refs_3_ = bf16[2,16,512]{2,1,0:T(8,128)(2,1)S(1)} collective-permute-done((bf16[2,16,512]{2,1,0:T(8,128)(2,1)S(1)}, bf16[2,16,512]{2,1,0:T(8,128)(2,1)S(1)}, u32[]{:S(2)}, u32[]{:S(2)}) %collective-permute-start.3) | collective-permute-done | bytes 32800 | tf_op jit(solution)/shard_map/ppermute | solution.py:107
  23.4 2.8 %collective-permute-done.2.refs_2_ = bf16[2,16,512]{2,1,0:T(8,128)(2,1)S(1)} collective-permute-done((bf16[2,16,512]{2,1,0:T(8,128)(2,1)S(1)}, bf16[2,16,512]{2,1,0:T(8,128)(2,1)S(1)}, u32[]{:S(2)}, u32[]{:S(2)}) %collective-permute-start.2) | collective-permute-done | bytes 32800 | tf_op jit(solution)/shard_map/ppermute | solution.py:107
  26.2 0.0 collective-permute-done.1.refs_1_
  26.2 0.0 collective-permute-done.5.refs_5_
  26.2 0.0 collective-permute-done.7.refs_7_
  26.2 1.7 %tile.1 = f32[512,1024]{1,0:T(8,128)} custom-call(bf16[2,16,512]{2,1,0:T(8,128)(2,1)S(1)} %fusion.refs_0_, bf16[2,16,512]{2,1,0:T(8,128)(2,1)S(1)} %collective-permute-done.1.refs_1_, bf16[2,16,512]{2,1,0:T(8,128)(2,1)S(1)} %collective-permute-done.2.refs_2_, bf16[2,16,512]{2,1,0:T(8,128)(2,1)S(1)} %collective-permute-done.3.refs_3_, ...), custom_call_target="tpu_custom_call" | custom-call | flops 134217728 | bytes 2097152 | tf_op jit(solution)/shard_map/tile/pallas_call | solution.py:191
  (3 shorter events, 0.0 us)
Async XLA Ops:
  0.0 3.4 %copy-start = (bf16[4096,1024]{1,0:T(8,128)(2,1)S(1)}, bf16[4096,1024]{1,0:T(8,128)(2,1)}, u32[]{:S(2)}) copy-start(bf16[4096,1024]{1,0:T(8,128)(2,1)} %basis.1) | copy-start | bytes 25165828
  3.4 0.9 %copy-start.1 = (bf16[2,16,4096]{2,1,0:T(8,128)(2,1)S(1)}, bf16[2,16,4096]{2,1,0:T(8,128)(2,1)}, u32[]{:S(2)}) copy-start(bf16[2,16,4096]{2,1,0:T(8,128)(2,1)} %param.5) | copy-start | bytes 786436
  4.3 10.6 %copy-start.2 = (s32[2]{0:T(128)S(1)}, s32[2]{0:T(128)}, u32[]{:S(2)}) copy-start(s32[2]{0:T(128)} %param.9) | copy-start | bytes 28
  5.9 6.9 %collective-permute-start.4 = (f32[2,16,1024]{2,1,0:T(8,128)S(1)}, f32[2,16,1024]{2,1,0:T(8,128)S(1)}, u32[]{:S(2)}, u32[]{:S(2)}) collective-permute-start(f32[2,16,1024]{2,1,0:T(8,128)S(1)} %bitcast.6), channel_id=1, source_target_pairs={{0,16},{16,0},{1,17},{17,1},{2,18},{18,2},{3,19},{19,3},{4,20},{20... | collective-permute-start | bytes 393224 | tf_op jit(solution)/shard_map/ppermute | solution.py:107
  12.7 4.5 %collective-permute-start = (f32[2,16,512]{2,1,0:T(8,128)S(1)}, f32[2,16,512]{2,1,0:T(8,128)S(1)}, u32[]{:S(2)}, u32[]{:S(2)}) collective-permute-start(f32[2,16,512]{2,1,0:T(8,128)S(1)} %constant_dynamic-slice_fusion), channel_id=1, source_target_pairs={{0,16},{16,0},{1,17},{17,1},{2,18},{18,2},{3,19},{19,3},{4,20},{20... | collective-permute-start | bytes 196616 | tf_op jit(solution)/shard_map/ppermute | solution.py:107
  12.8 4.3 %collective-permute-start.6 = (bf16[2,16,1024]{2,1,0:T(8,128)(2,1)S(1)}, bf16[2,16,1024]{2,1,0:T(8,128)(2,1)S(1)}, u32[]{:S(2)}, u32[]{:S(2)}) collective-permute-start(bf16[2,16,1024]{2,1,0:T(8,128)(2,1)S(1)} %add_convert_fusion.refs_4_), channel_id=1, source_target_pairs={{0,8},{4,12},{8,0},{12,4},{1,9},{5,13},{9,1},{13,5},{2,10},{6,14},... | collective-permute-start | bytes 196616 | tf_op jit(solution)/shard_map/ppermute | solution.py:107
  15.0 11.2 %collective-permute-start.5 = (bf16[2,16,1024]{2,1,0:T(8,128)(2,1)S(1)}, bf16[2,16,1024]{2,1,0:T(8,128)(2,1)S(1)}, u32[]{:S(2)}, u32[]{:S(2)}) collective-permute-start(bf16[2,16,1024]{2,1,0:T(8,128)(2,1)S(1)} %add_convert_fusion.refs_4_), channel_id=1, source_target_pairs={{0,4},{4,0},{8,12},{12,8},{1,5},{5,1},{9,13},{13,9},{2,6},{6,2},{1... | collective-permute-start | bytes 196616 | tf_op jit(solution)/shard_map/ppermute | solution.py:107
  17.2 9.0 %collective-permute-start.7 = (bf16[2,16,1024]{2,1,0:T(8,128)(2,1)S(1)}, bf16[2,16,1024]{2,1,0:T(8,128)(2,1)S(1)}, u32[]{:S(2)}, u32[]{:S(2)}) collective-permute-start(bf16[2,16,1024]{2,1,0:T(8,128)(2,1)S(1)} %collective-permute-done.6.refs_6_), channel_id=1, source_target_pairs={{0,4},{4,0},{8,12},{12,8},{1,5},{5,1},{9,13},{13,9},{2,6},{6,2},{1... | collective-permute-start | bytes 196616 | tf_op jit(solution)/shard_map/ppermute | solution.py:107
  17.2 6.2 %collective-permute-start.3 = (bf16[2,16,512]{2,1,0:T(8,128)(2,1)S(1)}, bf16[2,16,512]{2,1,0:T(8,128)(2,1)S(1)}, u32[]{:S(2)}, u32[]{:S(2)}) collective-permute-start(bf16[2,16,512]{2,1,0:T(8,128)(2,1)S(1)} %fusion.refs_0_), channel_id=1, source_target_pairs={{0,3},{1,2},{2,1},{3,0},{4,7},{5,6},{6,5},{7,4},{8,11},{9,10},{10,... | collective-permute-start | bytes 98312 | tf_op jit(solution)/shard_map/ppermute | solution.py:107
  21.3 4.8 %collective-permute-start.2 = (bf16[2,16,512]{2,1,0:T(8,128)(2,1)S(1)}, bf16[2,16,512]{2,1,0:T(8,128)(2,1)S(1)}, u32[]{:S(2)}, u32[]{:S(2)}) collective-permute-start(bf16[2,16,512]{2,1,0:T(8,128)(2,1)S(1)} %fusion.refs_0_), channel_id=1, source_target_pairs={{0,2},{1,3},{2,0},{3,1},{4,6},{5,7},{6,4},{7,5},{8,10},{9,11},{10,... | collective-permute-start | bytes 98312 | tf_op jit(solution)/shard_map/ppermute | solution.py:107
  21.3 4.8 %collective-permute-start.1 = (bf16[2,16,512]{2,1,0:T(8,128)(2,1)S(1)}, bf16[2,16,512]{2,1,0:T(8,128)(2,1)S(1)}, u32[]{:S(2)}, u32[]{:S(2)}) collective-permute-start(bf16[2,16,512]{2,1,0:T(8,128)(2,1)S(1)} %fusion.refs_0_), channel_id=1, source_target_pairs={{0,1},{1,0},{2,3},{3,2},{4,5},{5,4},{6,7},{7,6},{8,9},{9,8},{10,11... | collective-permute-start | bytes 98312 | tf_op jit(solution)/shard_map/ppermute | solution.py:107

commit v4 on v3

--- a/solution.py
+++ b/solution.py
@@ -147,7 +147,7 @@
     return terms + sent(terms, axis, 1)
 
 
-def tile_kernel(*refs, outs, ins, divisor):
+def tile_kernel(*refs, outs, ins, divisor, spans):
     out_pieces, in_pieces = refs[:outs], refs[outs : outs + ins]
     tile_hbm, kept, turned, tile, sems = refs[outs + ins :]
     for axis, pieces, whole in (("col", out_pieces, kept), ("row", in_pieces, turned)):
@@ -156,25 +156,27 @@
             slots = piece.shape[1]
             place = pl.multiple_of(source(len(pieces), own, k) * slots, slots)
             whole[:, pl.ds(place, slots), :] = piece[...]
-    steps, rows, _ = tile.shape
     writes = []
-    for step in range(steps):
+    first = 0
+    for step, rows in enumerate(spans):
+        place = slice(first, first + rows)
         total = None
         for n in range(kept.shape[0]):
             product = lax.dot_general(
-                kept[n, :, step * rows : (step + 1) * rows],
+                kept[n, :, place],
                 turned[n],
                 (((0,), (0,)), ((), ())),
                 preferred_element_type=jnp.float32,
             )
             square = product * product
             total = square if total is None else total + square
-        tile[step] = total * (1.0 / divisor) if paired(divisor) else total / divisor
+        tile[place] = total * (1.0 / divisor) if paired(divisor) else total / divisor
         write = pltpu.make_async_copy(
-            tile.at[step], tile_hbm.at[pl.ds(step * rows, rows)], sems.at[step]
+            tile.at[pl.ds(first, rows)], tile_hbm.at[pl.ds(first, rows)], sems.at[step]
         )
-        write.start()
+        write.start(priority=step % 2)
         writes.append(write)
+        first += rows
     for write in writes:
         write.wait()
 
@@ -183,14 +185,14 @@
     seqs, out_slots, rows = out_pieces[0].shape
     cols = in_pieces[0].shape[2]
     slot_total = out_slots * len(out_pieces)
-    steps = 4 if rows % 512 == 0 else 1
+    spans = [rows // 8] * 8 if rows % 512 == 0 else [rows]
     dtype = out_pieces[0].dtype
     pieces = [
         pltpu.with_memory_space_constraint(piece, pltpu.VMEM) for piece in out_pieces + in_pieces
     ]
     return pl.pallas_call(
         functools.partial(
-            tile_kernel, outs=len(out_pieces), ins=len(in_pieces), divisor=seqs * slot_total
+            tile_kernel, outs=len(out_pieces), ins=len(in_pieces), divisor=seqs * slot_total, spans=spans
         ),
         out_shape=jax.ShapeDtypeStruct((rows, cols), jnp.float32),
         in_specs=[pl.BlockSpec(memory_space=pltpu.VMEM)] * len(pieces),
@@ -198,8 +200,8 @@
         scratch_shapes=[
             pltpu.VMEM((seqs, slot_total, rows), dtype),
             pltpu.VMEM((seqs, slot_total, cols), dtype),
-            pltpu.VMEM((steps, rows // steps, cols), jnp.float32),
-            pltpu.SemaphoreType.DMA((steps,)),
+            pltpu.VMEM((rows, cols), jnp.float32),
+            pltpu.SemaphoreType.DMA((len(spans),)),
         ],
         cost_estimate=pl.CostEstimate(
             flops=2 * seqs * slot_total * rows * cols,

time: 28 us -> 28 us (level)
  no operation moved by 1% of the time
where the time goes in v4:
time: 28 us; the launch traced here: 27.8 us
  starting transfers between devices  9.9 us (35%)
  Pallas kernels  7.01 us (25%)
  waiting for transfers between devices  6.34 us (23%)
  local copies, waits for them, and re-layouts  4.35 us (16%)
    ppermute x8, starting transfers between devices, sent(): lax.ppermute(value, axis, [(i, target(size, i, step)) for i in range(size)])  9.9 us
    ppermute x8, waiting for transfers between devices, sent(): lax.ppermute(value, axis, [(i, target(size, i, step)) for i in range(size)])  6.34 us
    unnamed x6, local copies, waits for them, and re-layouts  4.33 us
    pallas_call x1, Pallas kernels, turned_terms(): pl.pallas_call(functools.partial(turning_kernel, spans=spans, ahead=AHEAD...  3.81 us
    pallas_call x1, Pallas kernels, tile_of(): pl.pallas_call(functools.partial(tile_kernel, outs=len(out_pieces), ins=l...  1.67 us
    pallas_call x1, Pallas kernels, held_terms(): pl.pallas_call(held_kernel, out_shape=pltpu.VMEM((rows, dirs), jnp.float3...  1.54 us
  transfers between devices with their start and end apart: 8, of which 3 were waited for; matrix products, arithmetic and copies ran while one was open for 1% of the time, Pallas kernels for 14%

profile of v4, /device:TPU:0, one launch (start us, length us, event | category | flops | bytes accessed | tf_op | source)
XLA Modules:
  0.0 27.8 jit_solution(11991067849183224086)
XLA Ops:
  0.0 0.0 copy-start
  0.0 3.4 %copy-done = bf16[4096,1024]{1,0:T(8,128)(2,1)S(1)} copy-done((bf16[4096,1024]{1,0:T(8,128)(2,1)S(1)}, bf16[4096,1024]{1,0:T(8,128)(2,1)}, u32[]{:S(2)}) %copy-start) | copy-done | bytes 8388632
  3.4 0.0 copy-start.1
  3.4 0.9 %copy-done.1 = bf16[2,16,4096]{2,1,0:T(8,128)(2,1)S(1)} copy-done((bf16[2,16,4096]{2,1,0:T(8,128)(2,1)S(1)}, bf16[2,16,4096]{2,1,0:T(8,128)(2,1)}, u32[]{:S(2)}) %copy-start.1) | copy-done | bytes 262168
  4.3 0.0 copy-start.2
  4.3 1.5 %held.1 = f32[32,1024]{1,0:T(8,128)S(1)} custom-call(bf16[32,4096]{1,0:T(8,128)(2,1)S(1)} %bitcast.8, bf16[4096,1024]{1,0:T(8,128)(2,1)S(1)} %copy-done), custom_call_target="tpu_custom_call" | custom-call | flops 268435456 | bytes 131072 | tf_op jit(solution)/shard_map/held/pallas_call | solution.py:76
  5.9 3.0 %collective-permute-start.4 = (f32[2,16,1024]{2,1,0:T(8,128)S(1)}, f32[2,16,1024]{2,1,0:T(8,128)S(1)}, u32[]{:S(2)}, u32[]{:S(2)}) collective-permute-start(f32[2,16,1024]{2,1,0:T(8,128)S(1)} %bitcast.6), channel_id=1, source_target_pairs={{0,16},{16,0},{1,17},{17,1},{2,18},{18,2},{3,19},{19,3},{4,20},{20... | collective-permute-start | bytes 393224 | tf_op jit(solution)/shard_map/ppermute | solution.py:107
  8.9 3.8 %turning.1 = f32[32,1024]{1,0:T(8,128)S(1)} custom-call(bf16[32,4096]{1,0:T(8,128)(2,1)} %bitcast.9, bf16[4096,1024]{1,0:T(8,128)(2,1)} %basis_hbm.1), custom_call_target="tpu_custom_call" | custom-call | flops 268435456 | bytes 8650752 | tf_op jit(solution)/shard_map/turning/pallas_call | solution.py:43
  12.7 0.1 collective-permute-start
  12.8 0.0 collective-permute-done.4
  12.8 2.1 %collective-permute-start.6 = (bf16[2,16,1024]{2,1,0:T(8,128)(2,1)S(1)}, bf16[2,16,1024]{2,1,0:T(8,128)(2,1)S(1)}, u32[]{:S(2)}, u32[]{:S(2)}) collective-permute-start(bf16[2,16,1024]{2,1,0:T(8,128)(2,1)S(1)} %add_convert_fusion.refs_4_), channel_id=1, source_target_pairs={{0,8},{4,12},{8,0},{12,4},{1,9},{5,13},{9,1},{13,5},{2,10},{6,14},... | collective-permute-start | bytes 196616 | tf_op jit(solution)/shard_map/ppermute | solution.py:107
  14.9 0.0 copy-done.2
  14.9 0.1 broadcast_compare_fusion
  15.0 0.0 collective-permute-start.5
  15.0 2.2 %collective-permute-done.6.refs_6_ = bf16[2,16,1024]{2,1,0:T(8,128)(2,1)S(1)} collective-permute-done((bf16[2,16,1024]{2,1,0:T(8,128)(2,1)S(1)}, bf16[2,16,1024]{2,1,0:T(8,128)(2,1)S(1)}, u32[]{:S(2)}, u32[]{:S(2)}) %collective-permute-start.6) | collective-permute-done | bytes 65568 | tf_op jit(solution)/shard_map/ppermute | solution.py:107
  17.2 0.0 collective-permute-start.7
  17.2 0.0 collective-permute-done
  17.2 0.1 fusion.refs_0_
  17.2 4.1 %collective-permute-start.3 = (bf16[2,16,512]{2,1,0:T(8,128)(2,1)S(1)}, bf16[2,16,512]{2,1,0:T(8,128)(2,1)S(1)}, u32[]{:S(2)}, u32[]{:S(2)}) collective-permute-start(bf16[2,16,512]{2,1,0:T(8,128)(2,1)S(1)} %fusion.refs_0_), channel_id=1, source_target_pairs={{0,3},{1,2},{2,1},{3,0},{4,7},{5,6},{6,5},{7,4},{8,11},{9,10},{10,... | collective-permute-start | bytes 98312 | tf_op jit(solution)/shard_map/ppermute | solution.py:107
  21.3 0.0 collective-permute-start.2
  21.3 0.6 %collective-permute-start.1 = (bf16[2,16,512]{2,1,0:T(8,128)(2,1)S(1)}, bf16[2,16,512]{2,1,0:T(8,128)(2,1)S(1)}, u32[]{:S(2)}, u32[]{:S(2)}) collective-permute-start(bf16[2,16,512]{2,1,0:T(8,128)(2,1)S(1)} %fusion.refs_0_), channel_id=1, source_target_pairs={{0,1},{1,0},{2,3},{3,2},{4,5},{5,4},{6,7},{7,6},{8,9},{9,8},{10,11... | collective-permute-start | bytes 98312 | tf_op jit(solution)/shard_map/ppermute | solution.py:107
  22.0 1.4 %collective-permute-done.3.refs_3_ = bf16[2,16,512]{2,1,0:T(8,128)(2,1)S(1)} collective-permute-done((bf16[2,16,512]{2,1,0:T(8,128)(2,1)S(1)}, bf16[2,16,512]{2,1,0:T(8,128)(2,1)S(1)}, u32[]{:S(2)}, u32[]{:S(2)}) %collective-permute-start.3) | collective-permute-done | bytes 32800 | tf_op jit(solution)/shard_map/ppermute | solution.py:107
  23.4 2.8 %collective-permute-done.2.refs_2_ = bf16[2,16,512]{2,1,0:T(8,128)(2,1)S(1)} collective-permute-done((bf16[2,16,512]{2,1,0:T(8,128)(2,1)S(1)}, bf16[2,16,512]{2,1,0:T(8,128)(2,1)S(1)}, u32[]{:S(2)}, u32[]{:S(2)}) %collective-permute-start.2) | collective-permute-done | bytes 32800 | tf_op jit(solution)/shard_map/ppermute | solution.py:107
  26.2 0.0 collective-permute-done.1.refs_1_
  26.2 0.0 collective-permute-done.5.refs_5_
  26.2 0.0 collective-permute-done.7.refs_7_
  26.2 1.7 %tile.1 = f32[512,1024]{1,0:T(8,128)} custom-call(bf16[2,16,512]{2,1,0:T(8,128)(2,1)S(1)} %fusion.refs_0_, bf16[2,16,512]{2,1,0:T(8,128)(2,1)S(1)} %collective-permute-done.1.refs_1_, bf16[2,16,512]{2,1,0:T(8,128)(2,1)S(1)} %collective-permute-done.2.refs_2_, bf16[2,16,512]{2,1,0:T(8,128)(2,1)S(1)} %collective-permute-done.3.refs_3_, ...), custom_call_target="tpu_custom_call" | custom-call | flops 134217728 | bytes 2097152 | tf_op jit(solution)/shard_map/tile/pallas_call | solution.py:193
  (3 shorter events, 0.0 us)
Async XLA Ops:
  0.0 3.4 %copy-start = (bf16[4096,1024]{1,0:T(8,128)(2,1)S(1)}, bf16[4096,1024]{1,0:T(8,128)(2,1)}, u32[]{:S(2)}) copy-start(bf16[4096,1024]{1,0:T(8,128)(2,1)} %basis.1) | copy-start | bytes 25165828
  3.4 0.9 %copy-start.1 = (bf16[2,16,4096]{2,1,0:T(8,128)(2,1)S(1)}, bf16[2,16,4096]{2,1,0:T(8,128)(2,1)}, u32[]{:S(2)}) copy-start(bf16[2,16,4096]{2,1,0:T(8,128)(2,1)} %param.5) | copy-start | bytes 786436
  4.3 10.6 %copy-start.2 = (s32[2]{0:T(128)S(1)}, s32[2]{0:T(128)}, u32[]{:S(2)}) copy-start(s32[2]{0:T(128)} %param.9) | copy-start | bytes 28
  5.9 6.9 %collective-permute-start.4 = (f32[2,16,1024]{2,1,0:T(8,128)S(1)}, f32[2,16,1024]{2,1,0:T(8,128)S(1)}, u32[]{:S(2)}, u32[]{:S(2)}) collective-permute-start(f32[2,16,1024]{2,1,0:T(8,128)S(1)} %bitcast.6), channel_id=1, source_target_pairs={{0,16},{16,0},{1,17},{17,1},{2,18},{18,2},{3,19},{19,3},{4,20},{20... | collective-permute-start | bytes 393224 | tf_op jit(solution)/shard_map/ppermute | solution.py:107
  12.7 4.5 %collective-permute-start = (f32[2,16,512]{2,1,0:T(8,128)S(1)}, f32[2,16,512]{2,1,0:T(8,128)S(1)}, u32[]{:S(2)}, u32[]{:S(2)}) collective-permute-start(f32[2,16,512]{2,1,0:T(8,128)S(1)} %constant_dynamic-slice_fusion), channel_id=1, source_target_pairs={{0,16},{16,0},{1,17},{17,1},{2,18},{18,2},{3,19},{19,3},{4,20},{20... | collective-permute-start | bytes 196616 | tf_op jit(solution)/shard_map/ppermute | solution.py:107
  12.8 4.3 %collective-permute-start.6 = (bf16[2,16,1024]{2,1,0:T(8,128)(2,1)S(1)}, bf16[2,16,1024]{2,1,0:T(8,128)(2,1)S(1)}, u32[]{:S(2)}, u32[]{:S(2)}) collective-permute-start(bf16[2,16,1024]{2,1,0:T(8,128)(2,1)S(1)} %add_convert_fusion.refs_4_), channel_id=1, source_target_pairs={{0,8},{4,12},{8,0},{12,4},{1,9},{5,13},{9,1},{13,5},{2,10},{6,14},... | collective-permute-start | bytes 196616 | tf_op jit(solution)/shard_map/ppermute | solution.py:107
  15.0 11.2 %collective-permute-start.5 = (bf16[2,16,1024]{2,1,0:T(8,128)(2,1)S(1)}, bf16[2,16,1024]{2,1,0:T(8,128)(2,1)S(1)}, u32[]{:S(2)}, u32[]{:S(2)}) collective-permute-start(bf16[2,16,1024]{2,1,0:T(8,128)(2,1)S(1)} %add_convert_fusion.refs_4_), channel_id=1, source_target_pairs={{0,4},{4,0},{8,12},{12,8},{1,5},{5,1},{9,13},{13,9},{2,6},{6,2},{1... | collective-permute-start | bytes 196616 | tf_op jit(solution)/shard_map/ppermute | solution.py:107
  17.2 9.0 %collective-permute-start.7 = (bf16[2,16,1024]{2,1,0:T(8,128)(2,1)S(1)}, bf16[2,16,1024]{2,1,0:T(8,128)(2,1)S(1)}, u32[]{:S(2)}, u32[]{:S(2)}) collective-permute-start(bf16[2,16,1024]{2,1,0:T(8,128)(2,1)S(1)} %collective-permute-done.6.refs_6_), channel_id=1, source_target_pairs={{0,4},{4,0},{8,12},{12,8},{1,5},{5,1},{9,13},{13,9},{2,6},{6,2},{1... | collective-permute-start | bytes 196616 | tf_op jit(solution)/shard_map/ppermute | solution.py:107
  17.2 6.2 %collective-permute-start.3 = (bf16[2,16,512]{2,1,0:T(8,128)(2,1)S(1)}, bf16[2,16,512]{2,1,0:T(8,128)(2,1)S(1)}, u32[]{:S(2)}, u32[]{:S(2)}) collective-permute-start(bf16[2,16,512]{2,1,0:T(8,128)(2,1)S(1)} %fusion.refs_0_), channel_id=1, source_target_pairs={{0,3},{1,2},{2,1},{3,0},{4,7},{5,6},{6,5},{7,4},{8,11},{9,10},{10,... | collective-permute-start | bytes 98312 | tf_op jit(solution)/shard_map/ppermute | solution.py:107
  21.3 4.8 %collective-permute-start.2 = (bf16[2,16,512]{2,1,0:T(8,128)(2,1)S(1)}, bf16[2,16,512]{2,1,0:T(8,128)(2,1)S(1)}, u32[]{:S(2)}, u32[]{:S(2)}) collective-permute-start(bf16[2,16,512]{2,1,0:T(8,128)(2,1)S(1)} %fusion.refs_0_), channel_id=1, source_target_pairs={{0,2},{1,3},{2,0},{3,1},{4,6},{5,7},{6,4},{7,5},{8,10},{9,11},{10,... | collective-permute-start | bytes 98312 | tf_op jit(solution)/shard_map/ppermute | solution.py:107
  21.3 4.8 %collective-permute-start.1 = (bf16[2,16,512]{2,1,0:T(8,128)(2,1)S(1)}, bf16[2,16,512]{2,1,0:T(8,128)(2,1)S(1)}, u32[]{:S(2)}, u32[]{:S(2)}) collective-permute-start(bf16[2,16,512]{2,1,0:T(8,128)(2,1)S(1)} %fusion.refs_0_), channel_id=1, source_target_pairs={{0,1},{1,0},{2,3},{3,2},{4,5},{5,4},{6,7},{7,6},{8,9},{9,8},{10,11... | collective-permute-start | bytes 98312 | tf_op jit(solution)/shard_map/ppermute | solution.py:107
